TPU v7x, 512 devices: a whole 4x4x16 slice. The times are simulated.
512 devices in a mesh: batch: 16 (over y, x), ctx: 32 (over z, core).
Axes of the slice: x: 4, y: 4, z: 16, core: 2. Of those that a mesh axis runs over, the one named last changes fastest.
Arguments:
- asked_for: bfloat16 [16, 4096, 64, 64], P('batch', 'ctx'), may hold values from -6 to 6
- offered: bfloat16 [16, 4096, 64, 64], P('batch', 'ctx'), may hold values from -6 to 6
- contents: bfloat16 [16, 4096, 64, 64], P('batch', 'ctx'), may hold values from -6 to 6
- out_weight: bfloat16 [4096, 4096], P('batch'), may hold values from -0.09375 to 0.09375
Outputs:
- layer_out: bfloat16 [16, 4096, 4096], P('batch', 'ctx')
All inputs are finite; a program needn't handle non-finite values.
Results may differ from a plain program's by a relative error of at most 0.006.
Values may be sent and summed in bfloat16 or wider, within the bound.
A program may use at most 128 MiB of HBM per device.

v0:
```python
import jax
import jax.numpy as jnp
from jax import lax
from jax.sharding import PartitionSpec as P


def packed_total(arrays, axis):
    ends = [0]
    for a in arrays:
        ends.append(ends[-1] + a.size)
    total = lax.psum(jnp.concatenate([a.ravel() for a in arrays]), axis)
    return tuple((total[b:e].reshape(a.shape) for a, b, e in zip(arrays, ends, ends[1:])))


def to_features(values):
    wide = values.astype(jnp.float32)
    return jax.nn.softplus(wide).astype(jnp.bfloat16)


def after_reading(read, count):
    result = read * count**0.5
    return result.astype(jnp.bfloat16)


def look_up(features, state, mass):
    top = jnp.einsum(
        "bthd,bhde->bthe", features, state.astype(jnp.bfloat16), preferred_element_type=jnp.float32
    )
    bottom = jnp.einsum("bthd,bhd->bth", features.astype(jnp.float32), mass)
    return top / (bottom + 0.001)[..., None]


def shards(asked_for, offered, contents, out_weight):
    query_feature, key_feature = (to_features(asked_for), to_features(offered))
    count = asked_for.shape[1] * lax.axis_size("ctx")
    part_state = jnp.einsum(
        "bthd,bthe->bhde", key_feature, contents, preferred_element_type=jnp.float32
    )
    part_mass = jnp.sum(key_feature.astype(jnp.float32), axis=1)
    state, mass = packed_total((part_state, part_mass), "ctx")
    read = look_up(query_feature, state / count, mass / count)
    mixed = after_reading(read, count)
    mixed = mixed.reshape(mixed.shape[0], mixed.shape[1], -1)
    return jnp.einsum(
        "btw,wv->btv",
        mixed,
        lax.all_gather(out_weight, "batch", axis=0, tiled=True),
        preferred_element_type=jnp.float32,
    ).astype(jnp.bfloat16)


def solution(mesh):
    in_specs = (
        P("batch", "ctx", None, None),
        P("batch", "ctx", None, None),
        P("batch", "ctx", None, None),
        P("batch", None),
    )
    out_specs = P("batch", "ctx", None)
    return jax.shard_map(shards, mesh=mesh, in_specs=in_specs, out_specs=out_specs, check_vma=False)
```

profile of v0, /device:TPU:1, one launch (start us, length us, event | category | flops | bytes accessed | tf_op | source)
XLA Modules:
  0.0 263.6 jit_solution(13410124035713011407)
XLA Ops:
  7.4 0.0 copy-start
  7.4 0.0 all-reduce.2.cloned.1.call-start
  7.4 2.6 convert_reduce_fusion
  10.0 0.0 copy-done
  10.0 3.9 %fusion.15 = f32[64,64,64]{2,1,0:T(8,128)} fusion(bf16[1,128,64,64]{1,3,2,0:T(8,128)(2,1)S(1)} %copy-done, bf16[1,128,64,64]{1,3,2,0:T(8,128)(2,1)} %param.5), kind=kOutput, calls=%fused_computation.26 | convolution fusion | flops 71303168 | bytes 3145728 | tf_op jit(solution)/shard_map/bthd,bthe->bhde/dot_general | solution.py:36
  13.8 1.8 reshape.70
  15.7 0.1 reshape.71
  15.7 1.1 pad_maximum_fusion
  16.8 0.0 all-reduce.2.cloned.1.call-update
  16.8 0.0 all-gather.2.cloned.1.call-start
  16.9 0.5 all-gather.2.cloned.1.call-update
  17.4 218.0 %all-reduce.2.cloned.1.call-done = f32[266240]{0:T(1024)} async-done(((f32[266240]{0:T(1024)}), f32[266240]{0:T(1024)}) %all-reduce.2.cloned.1.call-update) | async-done | bytes 1064976 | tf_op jit(solution)/shard_map/psum | solution.py:11
  235.4 1.3 fusion.14
  236.7 0.4 convert_element_type.38
  237.1 0.7 slice_multiply_fusion.1
  237.8 0.1 reshape.74
  237.9 0.0 copy-start.1
  237.9 2.6 fusion.19
  240.5 0.0 copy-done.1
  240.5 1.6 fusion.12
  242.1 0.0 all-gather.2.cloned.1.call-done
  242.1 14.0 %fusion = bf16[1,128,4096]{2,1,0:T(8,128)(2,1)} fusion(bf16[128,4096]{0,1:T(8,128)(2,1)S(1)} %bitcast.34, bf16[4096,4096]{1,0:T(8,128)(2,1)} %all-gather.2.cloned.1.call-done), kind=kOutput, calls=%fused_computation.3 | convolution fusion | flops 4295491584 | bytes 35651584 | tf_op jit(solution)/shard_map/btw,wv->btv/dot_general | solution.py:44
  (1 shorter events, 0.0 us)
Async XLA Ops:
  7.4 2.6 copy-start
  7.4 228.0 %all-reduce.2.cloned.1.call-start = ((), (), s32[]{:S(2)}) async-start(), calls=%async_computation | async-start | bytes 2129920 | tf_op jit(solution)/shard_map/psum | solution.py:11
  16.8 225.3 %all-gather.2.cloned.1.call-start = ((), (), s32[]{:S(2)}) async-start(), calls=%async_computation.1 | async-start | bytes 35651584 | tf_op jit(solution)/shard_map/all_gather | solution.py:47
  237.9 2.6 copy-start.1
Sparse Core Ops, SparseCore 0:
  17.0 218.3 all-reduce.1
Sparse Core Ops, SparseCore 1:
  20.3 217.2 all-gather.1
where the time goes:
time: 264 us
  waiting for transfers between devices  219 us (83%)
  matrix products  22.1 us (8%)
  between operations  14.9 us (6%)
  other arithmetic  5.7 us (2%)
    psum x1, waiting for transfers between devices, packed_total(): total = lax.psum(jnp.concatenate([a.ravel() for a in arrays]), axis)  218 us
    dot_general x1, matrix products, shards(): jnp.einsum('btw,wv->btv', mixed, lax.all_gather(out_weight, 'batch', axis...  14 us
  transfers between devices with their start and end apart: 2, of which 1 were waited for; matrix products, arithmetic and copies ran while one was open for 3% of the time, Pallas kernels for 0%

commit v1 on v0

--- a/solution.py
+++ b/solution.py
@@ -8,7 +8,9 @@
     ends = [0]
     for a in arrays:
         ends.append(ends[-1] + a.size)
-    total = lax.psum(jnp.concatenate([a.ravel() for a in arrays]), axis)
+    own = jnp.concatenate([a.ravel() for a in arrays])
+    parts = lax.all_gather(own, axis)
+    total = jnp.sum(parts, axis=0)
     return tuple((total[b:e].reshape(a.shape) for a, b, e in zip(arrays, ends, ends[1:])))
 
 

time: 264 us -> 447 us (1.69)
  waiting for transfers between devices: 219 us -> 356 us
  local copies, waits for them, and re-layouts: 2.35 us -> 35.3 us
  other arithmetic: 5.7 us -> 20.3 us
    psum x1 -> x0, waiting for transfers between devices: 218 us -> none  [packed_total(): total = lax.psum(jnp.concatenate([a.ravel() for a in arrays]), axis)]
    all_gather x0 -> x1, waiting for transfers between devices: none -> 199 us  [packed_total(): parts = lax.all_gather(own, axis)]
    all_gather x1, waiting for transfers between devices: 0.03 us -> 157 us  [shards(): lax.all_gather(out_weight, 'batch', axis=0, tiled=True)]
    all_gather x0 -> x1, local copies, waits for them, and re-layouts: none -> 34.4 us  [packed_total(): parts = lax.all_gather(own, axis)]
    reduce_sum x0 -> x1, other arithmetic: none -> 16.6 us  [packed_total(): total = jnp.sum(parts, axis=0)]
  transfers between devices with their start and end apart: 2 -> 2, of which waited for: 1 -> 2; matrix products, arithmetic and copies ran while one was open for 3% -> 12% of each run, Pallas kernels for 0% -> 0%
where the time goes in v1:
time: 447 us; the launch traced here: 446 us
  waiting for transfers between devices  356 us (80%)
  local copies, waits for them, and re-layouts  35.3 us (8%)
  matrix products  20.9 us (5%)
  other arithmetic  20.3 us (5%)
  between operations  13.5 us (3%)
    all_gather x1, waiting for transfers between devices, packed_total(): parts = lax.all_gather(own, axis)  199 us
    all_gather x1, waiting for transfers between devices, shards(): lax.all_gather(out_weight, 'batch', axis=0, tiled=True)  157 us
    all_gather x1, local copies, waits for them, and re-layouts, packed_total(): parts = lax.all_gather(own, axis)  34.4 us
    reduce_sum x1, other arithmetic, packed_total(): total = jnp.sum(parts, axis=0)  16.6 us
    dot_general x1, matrix products, shards(): jnp.einsum('btw,wv->btv', mixed, lax.all_gather(out_weight, 'batch', axis...  14.1 us
  transfers between devices with their start and end apart: 2, of which 2 were waited for; matrix products, arithmetic and copies ran while one was open for 12% of the time, Pallas kernels for 0%

profile of v1, /device:TPU:1, one launch (start us, length us, event | category | flops | bytes accessed | tf_op | source)
XLA Modules:
  0.0 446.4 jit_solution(1374833775931833841)
XLA Ops:
  6.5 0.0 copy-start
  6.5 0.0 all-gather.6.cloned.1.call-start
  6.5 2.6 convert_reduce_fusion
  9.1 0.0 copy-done
  9.1 2.5 fusion.15
  11.7 0.3 reshape.70
  12.0 0.1 reshape.71
  12.1 1.1 pad_maximum_fusion
  13.2 0.0 all-gather.6.cloned.1.call-update
  13.2 0.2 all-gather.4.cloned.1.call-start
  13.4 0.5 all-gather.4.cloned.1.call-update
  13.9 198.9 %all-gather.6.cloned.1.call-done = f32[8519680]{0:T(1024)} async-done(((f32[266240]{0:T(1024)}), f32[8519680]{0:T(1024)}) %all-gather.6.cloned.1.call-update) | async-done | bytes 34078736 | tf_op jit(solution)/shard_map/all_gather | solution.py:12
  212.8 34.4 %reshape.74 = f32[32,266240]{1,0:T(8,128)} reshape(f32[8519680]{0:T(1024)} %all-gather.6.cloned.1.call-done) | data formatting | bytes 68157440 | tf_op jit(solution)/shard_map/all_gather | solution.py:12
  247.2 16.6 %reduce_sum.19 = f32[266240]{0:T(1024)S(1)} reduce(f32[32,266240]{1,0:T(8,128)} %reshape.74, f32[]{:T(128)} %constant.4.clone.1), dimensions={0}, to_apply=%region_1.2 | reduce | flops 8253440 | bytes 35143684 | tf_op jit(solution)/shard_map/reduce_sum | solution.py:13
  263.8 0.1 fusion.14
  263.9 0.4 convert_element_type.38
  264.3 0.1 reshape.75
  264.4 0.0 copy-start.2
  264.4 2.6 fusion.19
  267.0 0.0 copy-done.2
  267.0 1.6 fusion.12
  268.6 156.8 %all-gather.4.cloned.1.call-done = bf16[4096,4096]{1,0:T(8,128)(2,1)} async-done(((bf16[256,4096]{1,0:T(8,128)(2,1)}), bf16[4096,4096]{1,0:T(8,128)(2,1)}) %all-gather.4.cloned.1.call-update) | async-done | bytes 33554448 | tf_op jit(solution)/shard_map/all_gather | solution.py:49
  425.4 0.0 copy-start.1
  425.4 14.1 %fusion = bf16[1,128,4096]{2,1,0:T(8,128)(2,1)} fusion(bf16[128,4096]{0,1:T(8,128)(2,1)S(1)} %bitcast.34, bf16[4096,4096]{1,0:T(8,128)(2,1)} %all-gather.4.cloned.1.call-done), kind=kOutput, calls=%fused_computation.3 | convolution fusion | flops 4295491584 | bytes 35651584 | tf_op jit(solution)/shard_map/btw,wv->btv/dot_general | solution.py:46
  439.6 0.0 copy-done.1
  (2 shorter events, 0.0 us)
Async XLA Ops:
  6.5 2.6 copy-start
  6.5 206.3 %all-gather.6.cloned.1.call-start = ((), (), s32[]{:S(2)}) async-start(), calls=%async_computation.1 | async-start | bytes 35143680 | tf_op jit(solution)/shard_map/all_gather | solution.py:12
  13.2 412.3 %all-gather.4.cloned.1.call-start = ((), (), s32[]{:S(2)}) async-start(), calls=%async_computation | async-start | bytes 35651584 | tf_op jit(solution)/shard_map/all_gather | solution.py:49
  264.4 2.6 copy-start.2
  425.4 14.1 %copy-start.1 = (bf16[1,128,64,64]{1,3,2,0:T(8,128)(2,1)S(1)}, bf16[1,128,64,64]{1,3,2,0:T(8,128)(2,1)}, u32[]{:S(2)}) copy-start(bf16[1,128,64,64]{1,3,2,0:T(8,128)(2,1)} %param.6) | copy-start | bytes 3145732
Sparse Core Ops, SparseCore 0:
  13.3 199.4 all-gather.5
  215.9 209.5 all-gather.3
